TPU v7x, 32 devices: a whole 2x2x4 slice. The times are simulated.
32 devices in a mesh: owner: 8 (over z, y), rows: 4 (over x, core).
Axes of the slice: x: 2, y: 2, z: 4, core: 2. Of those that a mesh axis runs over, the one named last changes fastest.
Arguments:
- master_down: float32 [16, 6400, 4096], P('owner', None, 'rows'), may hold values from -0.109375 to 0.109375
- router_weight: float32 [4096, 16], P('rows', 'owner'), may hold values from -0.09375 to 0.09375
- router_gain: float32 [4096], P('rows'), may hold values from 0.25 to 1.75
Outputs:
- final_down: bfloat16 [16, 6400, 4096], P('owner', 'rows')
- scale_down: float32 [16, 6400], P('owner', 'rows')
- serve_router: bfloat16 [4096, 16], replicated
All inputs are finite; a program needn't handle non-finite values. Where the computation divides by a largest or mean magnitude, that divisor is 1e-20 or more.
Results may differ from a plain program's by a relative error of at most 0.001.
Values may be sent and summed in bfloat16 or wider, within the bound.
A program may use at most 192 MiB of HBM per device.

v0:
```python
import jax
import jax.numpy as jnp
from jax import lax
from jax.sharding import PartitionSpec as P

D_MODEL = 4096


def per_device(master_down, router_weight, router_gain):
    total_down = lax.psum(jnp.sum(jnp.abs(master_down), axis=2), "rows")
    scale_down = total_down / D_MODEL
    narrow_down = (master_down / jnp.expand_dims(scale_down, 2)).astype(jnp.bfloat16)
    final_down = lax.all_to_all(narrow_down, "rows", split_axis=1, concat_axis=2, tiled=True)
    scale_down = lax.dynamic_slice_in_dim(
        scale_down, lax.axis_index("rows") * final_down.shape[1], final_down.shape[1], axis=1
    )
    part_router = (router_weight * router_gain[:, None]).astype(jnp.bfloat16)
    row_router = lax.all_gather(part_router, "rows", axis=0, tiled=True)
    serve_router = lax.all_gather(row_router, "owner", axis=1, tiled=True)
    return (final_down, scale_down, serve_router)


def solution(mesh):
    return jax.shard_map(
        per_device,
        mesh=mesh,
        in_specs=(P("owner", None, "rows"), P("rows", "owner"), P("rows")),
        out_specs=(P("owner", "rows", None), P("owner", "rows"), P()),
        check_vma=False,
    )
```

profile of v0, /device:TPU:0, one launch (start us, length us, event | category | flops | bytes accessed | tf_op | source)
XLA Modules:
  0.0 506.3 jit_solution(15090514093543817720)
XLA Ops:
  0.6 17.0 %abs_reduce_fusion = f32[2,6400]{1,0:T(2,128)S(1)} fusion(f32[2,6400,1024]{2,1,0:T(8,128)} %param.3), kind=kLoop, calls=%fused_computation.1 | loop fusion | flops 26201600 | bytes 52480000 | tf_op jit(solution)/shard_map/reduce_sum | solution.py:10
  17.6 13.4 %psum.7 = f32[2,6400]{1,0:T(2,128)S(1)} all-reduce(f32[2,6400]{1,0:T(2,128)S(1)} %abs_reduce_fusion), channel_id=1, replica_groups=mesh['owner'=8,'rows'=4] {'rows'}, use_global_device_ids=true, to_apply=%region_1.0 | all-reduce | flops 12800 | bytes 102400 | tf_op jit(solution)/shard_map/psum | solution.py:10
  31.1 26.1 %divide_convert_fusion = bf16[2,6400,1024]{2,1,0:T(8,128)(2,1)} fusion(f32[2,6400,1024]{2,1,0:T(8,128)} %param.3, f32[2,6400]{1,0:T(2,128)S(1)} %broadcast_multiply_fusion), kind=kLoop, calls=%fused_computation | loop fusion | flops 26214400 | bytes 78694400 | tf_op jit(solution)/shard_map/convert_element_type | solution.py:12
  57.2 0.0 copy-start
  57.2 0.0 copy-start.1
  57.2 47.4 %copy.10 = bf16[2,6400,1024]{2,0,1:T(2,128)(2,1)} copy(bf16[2,6400,1024]{2,1,0:T(8,128)(2,1)} %divide_convert_fusion) | data formatting | bytes 52428800 | tf_op jit(solution)/shard_map/convert_element_type | solution.py:12
  104.6 8.6 %all-to-all-start = ((bf16[2,6400,1024]{2,0,1:T(2,128)(2,1)}), bf16[2,6400,1024]{2,0,1:T(2,128)(2,1)}, u32[]{:S(2)}, u32[]{:S(2)}) async-start(bf16[2,6400,1024]{2,0,1:T(2,128)(2,1)} %copy.10), calls=%async_computation | async-start | bytes 52428800 | tf_op jit(solution)/shard_map/all_to_all | solution.py:13
  113.2 0.0 copy-done
  113.2 0.0 copy-done.1
  113.2 285.0 %all_gather.6 = bf16[4096,2]{0,1:T(2,128)(2,1)S(1)} all-gather(bf16[1024,2]{0,1:T(2,128)(2,1)S(1)} %multiply_convert_fusion), channel_id=1, replica_groups=mesh['owner'=8,'rows'=4] {'rows'}, dimensions={0}, use_global_device_ids=true | all-gather | bytes 20480 | tf_op jit(solution)/shard_map/all_gather | solution.py:18
  398.2 30.9 %all-gather = bf16[8,2,4096]{2,1,0:T(2,128)(2,1)S(1)} all-gather(bf16[1,2,4096]{2,1,0:T(2,128)(2,1)S(1)} %bitcast.8), channel_id=1, replica_groups=mesh['owner'=8,'rows'=4] {'owner'}, dimensions={0}, use_global_device_ids=true | all-gather | bytes 147456 | tf_op jit(solution)/shard_map/all_gather | solution.py:19
  429.1 0.7 reshape.9
  429.8 0.7 constant_dynamic-slice_fusion
  430.5 0.0 all-to-all-done
  430.5 33.4 %copy.11 = bf16[2,1600,4,1024]{3,2,1,0:T(4,128)(2,1)} copy(bf16[2,1600,4,1024]{3,0,1,2:T(2,128)(2,1)} %bitcast.1) | data formatting | bytes 52428800 | tf_op jit(solution)/shard_map/all_to_all | solution.py:13
  463.9 42.5 %all_to_all.16 = bf16[2,1600,4096]{2,1,0:T(8,128)(2,1)} reshape(bf16[2,1600,4,1024]{3,2,1,0:T(4,128)(2,1)} %copy.11) | data formatting | bytes 52428800 | tf_op jit(solution)/shard_map/all_to_all | solution.py:13
  (2 shorter events, 0.0 us)
Async XLA Ops:
  57.2 56.0 %copy-start = (f32[1024,2]{0,1:T(2,128)S(1)}, f32[1024,2]{0,1:T(2,128)}, u32[]{:S(2)}) copy-start(f32[1024,2]{0,1:T(2,128)} %param.4) | copy-start | bytes 24580
  57.2 56.0 %copy-start.1 = (f32[1024]{0:T(1024)S(1)}, f32[1024]{0:T(1024)}, u32[]{:S(2)}) copy-start(f32[1024]{0:T(1024)} %param.5) | copy-start | bytes 12292
  104.6 325.9 %all-to-all-start = ((bf16[2,6400,1024]{2,0,1:T(2,128)(2,1)}), bf16[2,6400,1024]{2,0,1:T(2,128)(2,1)}, u32[]{:S(2)}, u32[]{:S(2)}) async-start(bf16[2,6400,1024]{2,0,1:T(2,128)(2,1)} %copy.10), calls=%async_computation | async-start | bytes 52428800 | tf_op jit(solution)/shard_map/all_to_all | solution.py:13
where the time goes:
time: 508 us; the launch traced here: 506 us
  blocking collectives  329 us (65%)
  local copies, waits for them, and re-layouts  125 us (25%)
  other arithmetic  43.2 us (9%)
  starting transfers between devices  8.59 us (2%)
    all_gather x1, blocking collectives, per_device(): row_router = lax.all_gather(part_router, 'rows', axis=0, tiled=True)  285 us
    all_to_all x2, local copies, waits for them, and re-layouts, per_device(): lax.all_to_all(narrow_down, 'rows', split_axis=1, concat_axis=2, tiled=True)  75.8 us
    convert_element_type x1, local copies, waits for them, and re-layouts, per_device(): (master_down / jnp.expand_dims(scale_down, 2)).astype(jnp.bfloat16)  47.4 us
    all_gather x1, blocking collectives, per_device(): serve_router = lax.all_gather(row_router, 'owner', axis=1, tiled=True)  30.9 us
    convert_element_type x1, other arithmetic, per_device(): (master_down / jnp.expand_dims(scale_down, 2)).astype(jnp.bfloat16)  26.1 us
    reduce_sum x1, other arithmetic, per_device(): total_down = lax.psum(jnp.sum(jnp.abs(master_down), axis=2), 'rows')  17 us
    psum x1, blocking collectives, per_device(): total_down = lax.psum(jnp.sum(jnp.abs(master_down), axis=2), 'rows')  13.4 us
  transfers between devices with their start and end apart: 1, of which 0 were waited for; matrix products, arithmetic and copies ran while one was open for 0% of the time, Pallas kernels for 0%

commit v1 on v0

--- a/solution.py
+++ b/solution.py
@@ -10,7 +10,12 @@
     total_down = lax.psum(jnp.sum(jnp.abs(master_down), axis=2), "rows")
     scale_down = total_down / D_MODEL
     narrow_down = (master_down / jnp.expand_dims(scale_down, 2)).astype(jnp.bfloat16)
-    final_down = lax.all_to_all(narrow_down, "rows", split_axis=1, concat_axis=2, tiled=True)
+    final_down = jnp.concatenate(
+        lax.all_to_all(
+            jnp.stack(jnp.split(narrow_down, lax.axis_size("rows"), axis=1)), "rows", 0, 0
+        ),
+        axis=2,
+    )
     scale_down = lax.dynamic_slice_in_dim(
         scale_down, lax.axis_index("rows") * final_down.shape[1], final_down.shape[1], axis=1
     )

time: 508 us -> 425 us (0.84)
  local copies, waits for them, and re-layouts: 125 us -> 32.6 us
  other arithmetic: 43.2 us -> 53.7 us
    all_to_all x2 -> x0, local copies, waits for them, and re-layouts: 75.8 us -> none  [per_device(): lax.all_to_all(narrow_down, 'rows', split_axis=1, concat_axis=2, tiled=True)]
    convert_element_type x1 -> x0, local copies, waits for them, and re-layouts: 47.4 us -> none  [per_device(): (master_down / jnp.expand_dims(scale_down, 2)).astype(jnp.bfloat16)]
    reshape x0 -> x1, local copies, waits for them, and re-layouts: none -> 21.7 us  [per_device(): jnp.concatenate(lax.all_to_all(jnp.stack(jnp.split(narrow_down, lax.axis_...]
    another operation x0 -> x1, other arithmetic: none -> 10.5 us  [per_device(): jnp.stack(jnp.split(narrow_down, lax.axis_size('rows'), axis=1))]
    another operation x0 -> x1, local copies, waits for them, and re-layouts: none -> 9.52 us  [per_device(): jnp.stack(jnp.split(narrow_down, lax.axis_size('rows'), axis=1))]
where the time goes in v1:
time: 425 us
  blocking collectives  329 us (77%)
  other arithmetic  53.7 us (13%)
  local copies, waits for them, and re-layouts  32.6 us (8%)
  starting transfers between devices  8.72 us (2%)
    all_gather x1, blocking collectives, per_device(): row_router = lax.all_gather(part_router, 'rows', axis=0, tiled=True)  285 us
    all_gather x1, blocking collectives, per_device(): serve_router = lax.all_gather(row_router, 'owner', axis=1, tiled=True)  30.9 us
    convert_element_type x1, other arithmetic, per_device(): (master_down / jnp.expand_dims(scale_down, 2)).astype(jnp.bfloat16)  26.1 us
    reshape x1, local copies, waits for them, and re-layouts, per_device(): jnp.concatenate(lax.all_to_all(jnp.stack(jnp.split(narrow_down, lax.axis_...  21.7 us
    reduce_sum x1, other arithmetic, per_device(): total_down = lax.psum(jnp.sum(jnp.abs(master_down), axis=2), 'rows')  17 us
    psum x1, blocking collectives, per_device(): total_down = lax.psum(jnp.sum(jnp.abs(master_down), axis=2), 'rows')  13.4 us
    another operation x1, other arithmetic, per_device(): jnp.stack(jnp.split(narrow_down, lax.axis_size('rows'), axis=1))  10.5 us
    another operation x1, local copies, waits for them, and re-layouts, per_device(): jnp.stack(jnp.split(narrow_down, lax.axis_size('rows'), axis=1))  9.52 us
  transfers between devices with their start and end apart: 1, of which 0 were waited for; matrix products, arithmetic and copies ran while one was open for 0% of the time, Pallas kernels for 0%

profile of v1, /device:TPU:0, one launch (start us, length us, event | category | flops | bytes accessed | tf_op | source)
XLA Modules:
  0.0 425.0 jit_solution(6237450179818523184)
XLA Ops:
  0.6 17.0 %abs_reduce_fusion = f32[2,6400]{1,0:T(2,128)S(1)} fusion(f32[2,6400,1024]{2,1,0:T(8,128)} %param.3), kind=kLoop, calls=%fused_computation.1 | loop fusion | flops 26201600 | bytes 52480000 | tf_op jit(solution)/shard_map/reduce_sum | solution.py:10
  17.6 13.4 %psum.7 = f32[2,6400]{1,0:T(2,128)S(1)} all-reduce(f32[2,6400]{1,0:T(2,128)S(1)} %abs_reduce_fusion), channel_id=1, replica_groups=mesh['owner'=8,'rows'=4] {'rows'}, use_global_device_ids=true, to_apply=%region_1.0 | all-reduce | flops 12800 | bytes 102400 | tf_op jit(solution)/shard_map/psum | solution.py:10
  31.1 26.1 %divide_convert_fusion = bf16[2,6400,1024]{2,1,0:T(8,128)(2,1)} fusion(f32[2,6400,1024]{2,1,0:T(8,128)} %param.3, f32[2,6400]{1,0:T(2,128)S(1)} %broadcast_multiply_fusion), kind=kLoop, calls=%fused_computation | loop fusion | flops 26214400 | bytes 78694400 | tf_op jit(solution)/shard_map/convert_element_type | solution.py:12
  57.2 9.5 %slice_bitcast_fusion.3 = (bf16[1,2,1600,1024]{3,2,1,0:T(8,128)(2,1)S(1)}, bf16[1,2,1600,1024]{3,2,1,0:T(8,128)(2,1)S(1)}, bf16[1,2,1600,1024]{3,2,1,0:T(8,128)(2,1)S(1)}, bf16[1,2,1600,1024]{3,2,1,0:T(8,128)(2,1)S(1)}) fusion(bf16[2,6400,1024]{2,1,0:T(8,128)(2,1)} %divide_convert_fusion), kind=kLoop, calls=%fused_computation.6 | loop fusion | bytes 52428800 | tf_op jit(solution)/shard_map/stack | solution.py:15
  66.7 10.5 %pad_maximum_fusion = bf16[4,2,1600,1024]{3,2,1,0:T(8,128)(2,1)} fusion(bf16[1,2,1600,1024]{3,2,1,0:T(8,128)(2,1)S(1)} %get-tuple-element.4, bf16[1,2,1600,1024]{3,2,1,0:T(8,128)(2,1)S(1)} %get-tuple-element.5, bf16[1,2,1600,1024]{3,2,1,0:T(8,128)(2,1)S(1)} %get-tuple-element.6, bf16[1,2,1600,1024]{3,2,1,0:T(8,128)(2,1)S(1)} %get-tuple-element.3), kind=kLoop, calls=%fused_computation.2 | loop fusion | flops 39321600 | bytes 52428800 | tf_op jit(solution)/shard_map/stack | solution.py:15
  77.3 0.0 copy-start
  77.3 0.0 copy-start.1
  77.3 8.7 %all-to-all-start = ((bf16[4,2,1600,1024]{3,2,1,0:T(8,128)(2,1)}), bf16[4,2,1600,1024]{3,2,1,0:T(8,128)(2,1)}, u32[]{:S(2)}, u32[]{:S(2)}) async-start(bf16[4,2,1600,1024]{3,2,1,0:T(8,128)(2,1)} %pad_maximum_fusion), calls=%async_computation | async-start | bytes 52428800 | tf_op jit(solution)/shard_map/all_to_all | solution.py:14
  86.0 0.0 copy-done
  86.0 0.0 copy-done.1
  86.0 285.0 %all_gather.6 = bf16[4096,2]{0,1:T(2,128)(2,1)S(1)} all-gather(bf16[1024,2]{0,1:T(2,128)(2,1)S(1)} %multiply_convert_fusion), channel_id=1, replica_groups=mesh['owner'=8,'rows'=4] {'rows'}, dimensions={0}, use_global_device_ids=true | all-gather | bytes 20480 | tf_op jit(solution)/shard_map/all_gather | solution.py:23
  371.1 30.9 %all-gather = bf16[8,2,4096]{2,1,0:T(2,128)(2,1)S(1)} all-gather(bf16[1,2,4096]{2,1,0:T(2,128)(2,1)S(1)} %bitcast.17), channel_id=1, replica_groups=mesh['owner'=8,'rows'=4] {'owner'}, dimensions={0}, use_global_device_ids=true | all-gather | bytes 147456 | tf_op jit(solution)/shard_map/all_gather | solution.py:24
  401.9 0.7 reshape.17
  402.6 0.7 constant_dynamic-slice_fusion
  403.3 0.0 all-to-all-done
  403.3 21.7 %copy.8 = bf16[4,2,200,8,1024]{4,3,0,2,1:T(8,128)(2,1)} copy(bf16[4,2,200,8,1024]{4,3,2,1,0:T(8,128)(2,1)} %bitcast.9) | data formatting | bytes 52428800 | tf_op jit(solution)/shard_map/reshape | solution.py:13
  (2 shorter events, 0.0 us)
Async XLA Ops:
  77.3 8.7 %copy-start = (f32[1024,2]{0,1:T(2,128)S(1)}, f32[1024,2]{0,1:T(2,128)}, u32[]{:S(2)}) copy-start(f32[1024,2]{0,1:T(2,128)} %param.4) | copy-start | bytes 24580
  77.3 8.7 %copy-start.1 = (f32[1024]{0:T(1024)S(1)}, f32[1024]{0:T(1024)}, u32[]{:S(2)}) copy-start(f32[1024]{0:T(1024)} %param.5) | copy-start | bytes 12292
  77.3 326.1 %all-to-all-start = ((bf16[4,2,1600,1024]{3,2,1,0:T(8,128)(2,1)}), bf16[4,2,1600,1024]{3,2,1,0:T(8,128)(2,1)}, u32[]{:S(2)}, u32[]{:S(2)}) async-start(bf16[4,2,1600,1024]{3,2,1,0:T(8,128)(2,1)} %pad_maximum_fusion), calls=%async_computation | async-start | bytes 52428800 | tf_op jit(solution)/shard_map/all_to_all | solution.py:14

commit v2 on v0

--- a/solution.py
+++ b/solution.py
@@ -15,7 +15,9 @@
         scale_down, lax.axis_index("rows") * final_down.shape[1], final_down.shape[1], axis=1
     )
     part_router = (router_weight * router_gain[:, None]).astype(jnp.bfloat16)
-    row_router = lax.all_gather(part_router, "rows", axis=0, tiled=True)
+    row_router = jnp.concatenate(
+        lax.all_to_all(jnp.stack([part_router] * lax.axis_size("rows")), "rows", 0, 0), axis=0
+    )
     serve_router = lax.all_gather(row_router, "owner", axis=1, tiled=True)
     return (final_down, scale_down, serve_router)
 

time: 508 us -> 479 us (0.943)
  blocking collectives: 329 us -> 43.7 us
  waiting for transfers between devices: 0.01 us -> 251 us
    all_gather x1 -> x0, blocking collectives: 285 us -> none  [per_device(): row_router = lax.all_gather(part_router, 'rows', axis=0, tiled=True)]
    all_to_all x1, waiting for transfers between devices: 0.01 us -> 251 us  [per_device(): lax.all_to_all(narrow_down, 'rows', split_axis=1, concat_axis=2, tiled=True)]
  transfers between devices with their start and end apart: 1 -> 2, of which waited for: 0 -> 1; matrix products, arithmetic and copies ran while one was open for 0% -> 19% of each run, Pallas kernels for 0% -> 0%
where the time goes in v2:
time: 479 us; the launch traced here: 478 us
  waiting for transfers between devices  251 us (52%)
  local copies, waits for them, and re-layouts  125 us (26%)
  other arithmetic  43.9 us (9%)
  blocking collectives  43.7 us (9%)
  starting transfers between devices  12.8 us (3%)
    all_to_all x1, waiting for transfers between devices, per_device(): lax.all_to_all(narrow_down, 'rows', split_axis=1, concat_axis=2, tiled=True)  251 us
    all_to_all x2, local copies, waits for them, and re-layouts, per_device(): lax.all_to_all(narrow_down, 'rows', split_axis=1, concat_axis=2, tiled=True)  75.8 us
    convert_element_type x1, local copies, waits for them, and re-layouts, per_device(): (master_down / jnp.expand_dims(scale_down, 2)).astype(jnp.bfloat16)  47.3 us
    all_gather x1, blocking collectives, per_device(): serve_router = lax.all_gather(row_router, 'owner', axis=1, tiled=True)  31.4 us
    convert_element_type x1, other arithmetic, per_device(): (master_down / jnp.expand_dims(scale_down, 2)).astype(jnp.bfloat16)  26.1 us
    reduce_sum x1, other arithmetic, per_device(): total_down = lax.psum(jnp.sum(jnp.abs(master_down), axis=2), 'rows')  17 us
    psum x1, blocking collectives, per_device(): total_down = lax.psum(jnp.sum(jnp.abs(master_down), axis=2), 'rows')  12.3 us
  transfers between devices with their start and end apart: 2, of which 1 were waited for; matrix products, arithmetic and copies ran while one was open for 19% of the time, Pallas kernels for 0%

profile of v2, /device:TPU:0, one launch (start us, length us, event | category | flops | bytes accessed | tf_op | source)
XLA Modules:
  0.0 477.7 jit_solution(16169897027497116059)
XLA Ops:
  0.6 0.7 multiply_convert_fusion
  1.3 0.6 stack.2
  2.0 4.2 all-to-all-start.1
  6.2 17.0 %abs_reduce_fusion = f32[2,6400]{1,0:T(2,128)S(1)} fusion(f32[2,6400,1024]{2,1,0:T(8,128)} %param.3), kind=kLoop, calls=%fused_computation.1 | loop fusion | flops 26201600 | bytes 52480000 | tf_op jit(solution)/shard_map/reduce_sum | solution.py:10
  23.2 12.3 %psum.7 = f32[2,6400]{1,0:T(2,128)S(1)} all-reduce(f32[2,6400]{1,0:T(2,128)S(1)} %abs_reduce_fusion), channel_id=1, replica_groups=mesh['owner'=8,'rows'=4] {'rows'}, use_global_device_ids=true, to_apply=%region_1.0 | all-reduce | flops 12800 | bytes 102400 | tf_op jit(solution)/shard_map/psum | solution.py:10
  35.6 26.1 %divide_convert_fusion = bf16[2,6400,1024]{2,1,0:T(8,128)(2,1)} fusion(f32[2,6400,1024]{2,1,0:T(8,128)} %param.3, f32[2,6400]{1,0:T(2,128)S(1)} %broadcast_multiply_fusion), kind=kLoop, calls=%fused_computation | loop fusion | flops 26214400 | bytes 78694400 | tf_op jit(solution)/shard_map/convert_element_type | solution.py:12
  61.7 47.3 %copy.10 = bf16[2,6400,1024]{2,0,1:T(2,128)(2,1)} copy(bf16[2,6400,1024]{2,1,0:T(8,128)(2,1)} %divide_convert_fusion) | data formatting | bytes 52428800 | tf_op jit(solution)/shard_map/convert_element_type | solution.py:12
  109.1 0.0 all-to-all-done.1
  109.1 8.6 %all-to-all-start = ((bf16[2,6400,1024]{2,0,1:T(2,128)(2,1)}), bf16[2,6400,1024]{2,0,1:T(2,128)(2,1)}, u32[]{:S(2)}, u32[]{:S(2)}) async-start(bf16[2,6400,1024]{2,0,1:T(2,128)(2,1)} %copy.10), calls=%async_computation | async-start | bytes 52428800 | tf_op jit(solution)/shard_map/all_to_all | solution.py:13
  117.7 0.7 constant_dynamic-slice_fusion
  118.4 31.4 %all-gather = bf16[8,2,4096]{2,1,0:T(2,128)(2,1)S(1)} all-gather(bf16[1,2,4096]{2,1,0:T(2,128)(2,1)S(1)} %bitcast.10), channel_id=1, replica_groups=mesh['owner'=8,'rows'=4] {'owner'}, dimensions={0}, use_global_device_ids=true | all-gather | bytes 147456 | tf_op jit(solution)/shard_map/all_gather | solution.py:21
  149.7 0.7 reshape.15
  150.5 251.4 %all-to-all-done = bf16[2,6400,1024]{2,0,1:T(2,128)(2,1)} async-done(((bf16[2,6400,1024]{2,0,1:T(2,128)(2,1)}), bf16[2,6400,1024]{2,0,1:T(2,128)(2,1)}, u32[]{:S(2)}, u32[]{:S(2)}) %all-to-all-start) | async-done | bytes 26214432 | tf_op jit(solution)/shard_map/all_to_all | solution.py:13
  401.8 33.3 %copy.11 = bf16[2,1600,4,1024]{3,2,1,0:T(4,128)(2,1)} copy(bf16[2,1600,4,1024]{3,0,1,2:T(2,128)(2,1)} %bitcast.1) | data formatting | bytes 52428800 | tf_op jit(solution)/shard_map/all_to_all | solution.py:13
  435.2 42.5 %all_to_all.19 = bf16[2,1600,4096]{2,1,0:T(8,128)(2,1)} reshape(bf16[2,1600,4,1024]{3,2,1,0:T(4,128)(2,1)} %copy.11) | data formatting | bytes 52428800 | tf_op jit(solution)/shard_map/all_to_all | solution.py:13
  (1 shorter events, 0.0 us)
Async XLA Ops:
  2.0 107.1 %all-to-all-start.1 = ((bf16[4,1024,2]{1,2,0:T(2,128)(2,1)}), bf16[4,1024,2]{1,2,0:T(2,128)(2,1)S(1)}, u32[]{:S(2)}, u32[]{:S(2)}) async-start(bf16[4,1024,2]{1,2,0:T(2,128)(2,1)} %stack.2), calls=%async_computation.1 | async-start | bytes 32768 | tf_op jit(solution)/shard_map/all_to_all | solution.py:19
  109.1 292.8 %all-to-all-start = ((bf16[2,6400,1024]{2,0,1:T(2,128)(2,1)}), bf16[2,6400,1024]{2,0,1:T(2,128)(2,1)}, u32[]{:S(2)}, u32[]{:S(2)}) async-start(bf16[2,6400,1024]{2,0,1:T(2,128)(2,1)} %copy.10), calls=%async_computation | async-start | bytes 52428800 | tf_op jit(solution)/shard_map/all_to_all | solution.py:13
